TPU v7x, 16 devices: a 4x2x1 block of a 4x4x8 slice. The times are simulated.
16 devices in a mesh: dp: 2 (over y, z), tp: 8 (over x, core).
Axes of the slice: x: 4, y: 2, z: 1, core: 2. Of those that a mesh axis runs over, the one named last changes fastest.
The devices are a block of a 4x4x8 slice.
Arguments:
- x_tokens: bfloat16 [32, 512, 3072], P('dp', 'tp'), parts along dimension 0
- e_time: float32 [32, 3, 3072], P('dp'), parts along dimension 0
- m_block: float32 [3, 3072], replicated
- w_q: bfloat16 [3072, 3072], P(None, 'tp')
- b_q: float32 [3072], P('tp')
- w_k: bfloat16 [3072, 3072], P(None, 'tp')
- b_k: float32 [3072], P('tp')
- w_v: bfloat16 [3072, 3072], P(None, 'tp')
- b_v: float32 [3072], P('tp')
- w_o: bfloat16 [3072, 3072], P('tp')
- b_o: float32 [3072], replicated
- g_q: float32 [3072], P('tp')
- g_k: float32 [3072], P('tp')
- positions: int32 [1024, 3], P('dp'), parts along dimension 0
- d_out: bfloat16 [32, 512, 3072], P('dp', 'tp'), parts along dimension 0
Outputs:
- output 1: bfloat16 [32, 512, 3072], P('dp', 'tp'), parts along dimension 0
- output 2: bfloat16 [32, 512, 3072], P('dp', 'tp'), parts along dimension 0
- output 3: float32 [32, 3, 3072], P('dp'), parts along dimension 0
- output 4: float32 [6, 3072], P('dp'), parts along dimension 0
- output 5: bfloat16 [6144, 3072], P('dp', 'tp'), parts along dimension 0
- output 6: bfloat16 [6144, 3072], P('dp', 'tp'), parts along dimension 0
- output 7: bfloat16 [6144, 3072], P('dp', 'tp'), parts along dimension 0
- output 8: bfloat16 [6144, 3072], P(('dp', 'tp')), parts along dimension 0
- output 9: float32 [6144], P(('dp', 'tp')), parts along dimension 0
- output 10: float32 [6144], P(('dp', 'tp')), parts along dimension 0
There are 2 independent parts. A program takes and returns all parts, laid end to end along the dimension named above; an argument that names none is the same for every part.
All inputs are finite; a program needn't handle non-finite values.
Results may differ from a plain program's by a relative error of at most 0.02.
Values are sent between devices in bfloat16 or wider.
A program may use at most 768 MiB of HBM per device.

v0:
```python
import jax
import jax.numpy as jnp
from jax import lax
from jax.sharding import PartitionSpec as P

HEAD_DIM = 128
EPS_NORM = 1e-6
ROPE_BASE = 10000.0
ROW_CONTRACT = (((0,), (0,)), ((), ()))
COL_CONTRACT = (((1,), (1,)), ((), ()))


def rope_angles(positions):
    half_dim = HEAD_DIM // 2
    side_len = HEAD_DIM // 6
    first_len = half_dim - 2 * side_len
    pair_idx = jnp.arange(half_dim)
    section = (pair_idx >= first_len).astype(jnp.int32) + (pair_idx >= first_len + side_len).astype(jnp.int32)
    offset = jnp.where(section == 0, 0, jnp.where(section == 1, first_len, first_len + side_len))
    sec_width = jnp.where(section == 0, first_len, side_len)
    freq_vals = ROPE_BASE ** (-(pair_idx - offset).astype(jnp.float32) / sec_width.astype(jnp.float32))
    select = jnp.where(section[None, :] == jnp.arange(3)[:, None], freq_vals[None, :], 0.0)
    angles = jnp.sum(positions.astype(jnp.float32)[:, :, None] * select[None, :, :], axis=1)
    return jnp.cos(angles), jnp.sin(angles)


def rope_rotate(values, cos_part, sin_part):
    val_pairs = values.reshape(values.shape[:-1] + (values.shape[-1] // 2, 2))
    even_part = val_pairs[..., 0]
    odd_part = val_pairs[..., 1]
    rotated = jnp.stack([even_part * cos_part - odd_part * sin_part, even_part * sin_part + odd_part * cos_part], axis=-1)
    return rotated.reshape(values.shape)


def attend(q_rot, k_rot, v_heads):
    scores = jnp.einsum('bqhd,bkhd->bhqk', q_rot, k_rot, preferred_element_type=jnp.float32) * HEAD_DIM ** -0.5
    attn_probs = jax.nn.softmax(scores, axis=-1).astype(jnp.bfloat16)
    return jnp.einsum('bhqk,bkhd->bqhd', attn_probs, v_heads, preferred_element_type=jnp.float32).astype(jnp.bfloat16)


def solution(mesh):
    tp_size = mesh.shape['tp']

    def device_step(x_loc, e_loc, m_block, w_q, b_q, w_k, b_k, w_v, b_v, w_o, b_o, g_q, g_k, pos_part, dy_loc):
        batch_size, seq_loc, model_dim = x_loc.shape
        seq_len = seq_loc * tp_size
        rows_all = batch_size * seq_len
        heads_loc = w_q.shape[1] // HEAD_DIM
        head_shape = (batch_size, seq_len, heads_loc, HEAD_DIM)
        cos_tab, sin_tab = rope_angles(pos_part)
        cos_bcast = cos_tab[None, :, None, :]
        sin_bcast = sin_tab[None, :, None, :]

        mod_rows = m_block[None] + e_loc
        shift_row = mod_rows[:, 0][:, None]
        scale_one = 1.0 + mod_rows[:, 1][:, None]
        gate_row = mod_rows[:, 2][:, None]
        x_float = x_loc.astype(jnp.float32)
        centered = x_float - jnp.mean(x_float, axis=-1, keepdims=True)
        inv_std = lax.rsqrt(jnp.mean(centered * centered, axis=-1, keepdims=True) + EPS_NORM)
        x_norm = centered * inv_std
        y_loc = (x_norm * scale_one + shift_row).astype(jnp.bfloat16)
        y_full = lax.all_gather(y_loc, 'tp', axis=1, tiled=True).reshape(rows_all, model_dim)

        q_raw = jnp.dot(y_full, w_q, preferred_element_type=jnp.float32) + b_q
        k_raw = jnp.dot(y_full, w_k, preferred_element_type=jnp.float32) + b_k
        v_heads = (jnp.dot(y_full, w_v, preferred_element_type=jnp.float32) + b_v).astype(jnp.bfloat16).reshape(head_shape)
        sq_sums = lax.psum(jnp.stack([jnp.sum(q_raw * q_raw, axis=-1), jnp.sum(k_raw * k_raw, axis=-1)]), 'tp')
        inv_rms = lax.rsqrt(sq_sums / model_dim + EPS_NORM)[:, :, None]
        q_hat = q_raw * inv_rms[0]
        k_hat = k_raw * inv_rms[1]
        q_rot = rope_rotate((q_hat * g_q).reshape(head_shape), cos_bcast, sin_bcast).astype(jnp.bfloat16)
        k_rot = rope_rotate((k_hat * g_k).reshape(head_shape), cos_bcast, sin_bcast).astype(jnp.bfloat16)
        attn_out, attn_pull = jax.vjp(attend, q_rot, k_rot, v_heads)
        o_flat = attn_out.reshape(rows_all, heads_loc * HEAD_DIM)
        part_sum = jnp.dot(o_flat, w_o, preferred_element_type=jnp.float32).astype(jnp.bfloat16).reshape(batch_size, seq_len, model_dim)
        proj_loc = lax.psum_scatter(part_sum, 'tp', scatter_dimension=1, tiled=True).astype(jnp.float32) + b_o
        x_out = (x_float + gate_row * proj_loc).astype(jnp.bfloat16)

        dy_float = dy_loc.astype(jnp.float32)
        d_gate = jnp.sum(dy_float * proj_loc, axis=1)
        d_proj = lax.all_gather((dy_float * gate_row).astype(jnp.bfloat16), 'tp', axis=1, tiled=True).reshape(rows_all, model_dim)
        d_wo = lax.dot_general(o_flat, d_proj, ROW_CONTRACT, preferred_element_type=jnp.float32).astype(jnp.bfloat16)
        d_attn = lax.dot_general(d_proj, w_o, COL_CONTRACT, preferred_element_type=jnp.float32).astype(jnp.bfloat16).reshape(head_shape)
        dq_rot, dk_rot, dv_heads = attn_pull(d_attn)
        dq_hat = rope_rotate(dq_rot.astype(jnp.float32), cos_bcast, -sin_bcast).reshape(rows_all, -1)
        dk_hat = rope_rotate(dk_rot.astype(jnp.float32), cos_bcast, -sin_bcast).reshape(rows_all, -1)
        d_gq = jnp.sum(dq_hat * q_hat, axis=0)
        d_gk = jnp.sum(dk_hat * k_hat, axis=0)
        dq_scaled = dq_hat * g_q
        dk_scaled = dk_hat * g_k
        stat_grads = lax.psum(jnp.stack([jnp.sum(dq_scaled * q_hat, axis=-1), jnp.sum(dk_scaled * k_hat, axis=-1)]), 'tp')[:, :, None] / model_dim
        dq_raw = (inv_rms[0] * (dq_scaled - q_hat * stat_grads[0])).astype(jnp.bfloat16)
        dk_raw = (inv_rms[1] * (dk_scaled - k_hat * stat_grads[1])).astype(jnp.bfloat16)
        dv_flat = dv_heads.reshape(rows_all, -1)
        d_wq = lax.dot_general(y_full, dq_raw, ROW_CONTRACT, preferred_element_type=jnp.float32).astype(jnp.bfloat16)
        d_wk = lax.dot_general(y_full, dk_raw, ROW_CONTRACT, preferred_element_type=jnp.float32).astype(jnp.bfloat16)
        d_wv = lax.dot_general(y_full, dv_flat, ROW_CONTRACT, preferred_element_type=jnp.float32).astype(jnp.bfloat16)
        dy_part = (lax.dot_general(dq_raw, w_q, COL_CONTRACT, preferred_element_type=jnp.float32)
                   + lax.dot_general(dk_raw, w_k, COL_CONTRACT, preferred_element_type=jnp.float32)
                   + lax.dot_general(dv_flat, w_v, COL_CONTRACT, preferred_element_type=jnp.float32))
        dy_part = dy_part.astype(jnp.bfloat16).reshape(batch_size, seq_len, model_dim)
        d_y = lax.psum_scatter(dy_part, 'tp', scatter_dimension=1, tiled=True).astype(jnp.float32)
        d_mod = lax.psum(jnp.stack([jnp.sum(d_y, axis=1), jnp.sum(d_y * x_norm, axis=1), d_gate], axis=1), 'tp')
        d_norm = d_y * scale_one
        d_x = dy_float + inv_std * (d_norm - jnp.mean(d_norm, axis=-1, keepdims=True) - x_norm * jnp.mean(d_norm * x_norm, axis=-1, keepdims=True))
        return (x_out, d_x.astype(jnp.bfloat16), d_mod, jnp.sum(d_mod, axis=0), d_wq, d_wk, d_wv, d_wo, d_gq, d_gk)

    in_specs = (P('dp', 'tp', None), P('dp', None, None), P(None, None), P(None, 'tp'), P('tp'), P(None, 'tp'), P('tp'),
                P(None, 'tp'), P('tp'), P('tp', None), P(None), P('tp'), P('tp'), P('dp', None), P('dp', 'tp', None))
    out_specs = (P('dp', 'tp', None), P('dp', 'tp', None), P('dp', None, None), P('dp', None), P('dp', 'tp'), P('dp', 'tp'),
                 P('dp', 'tp'), P(('dp', 'tp'), None), P(('dp', 'tp')), P(('dp', 'tp')))
    return jax.shard_map(device_step, mesh=mesh, in_specs=in_specs, out_specs=out_specs, check_vma=False)
```

profile of v0, /device:TPU:112, one launch (start us, length us, event | category | flops | bytes accessed | tf_op | source)
XLA Modules:
  0.0 1734.2 jit_solution(15508602226853692195)
XLA Ops:
  33.5 216.3 %all-gather.3.cloned.1.call-done = bf16[16,512,3072]{2,1,0:T(8,128)(2,1)} async-done(((bf16[16,64,3072]{2,1,0:T(8,128)(2,1)}), bf16[16,512,3072]{2,1,0:T(8,128)(2,1)}) %all-gather.3.cloned.1.call-update) | async-done | bytes 50331664 | tf_op jit(solution)/shard_map/all_gather | solution.py:63
  249.9 27.8 %multiply_reduce_fusion.5 = (f32[8192]{0:T(1024)S(1)}, f32[8192,384]{0,1:T(8,128)}) fusion(f32[384]{0:T(512)S(1)} %copy-done.30, bf16[8192,3072]{1,0:T(8,128)(2,1)} %bitcast.140, bf16[3072,384]{1,0:T(8,128)(2,1)S(1)} %copy-done), kind=kOutput, calls=%fused_computation.55 | convolution fusion | flops 19336781824 | bytes 65308160 | tf_op jit(solution)/shard_map/dot_general | solution.py:66
  277.7 29.1 %multiply_reduce_fusion.6 = (f32[8192]{0:T(1024)S(1)}, f32[8192,384]{0,1:T(8,128)}) fusion(f32[384]{0:T(512)S(1)} %copy-done.31, bf16[8192,3072]{1,0:T(8,128)(2,1)} %bitcast.141, bf16[3072,384]{1,0:T(8,128)(2,1)} %param.18), kind=kOutput, calls=%fused_computation.56 | convolution fusion | flops 19336781824 | bytes 65308160 | tf_op jit(solution)/shard_map/dot_general | solution.py:65
  307.4 33.7 %add_convert_fusion.1 = bf16[8192,384]{1,0:T(8,128)(2,1)} fusion(bf16[8192,3072]{1,0:T(8,128)(2,1)} %bitcast.142, bf16[3072,384]{1,0:T(8,128)(2,1)} %param.22, f32[384]{0:T(512)S(1)} %copy-done.32), kind=kOutput, calls=%fused_computation.57 | convolution fusion | flops 19333644288 | bytes 58983936 | tf_op jit(solution)/shard_map/dot_general | solution.py:67
  341.3 134.0 %all-gather.5.cloned.1.call-done = bf16[16,512,3072]{2,1,0:T(8,128)(2,1)} async-done(((bf16[16,64,3072]{2,1,0:T(8,128)(2,1)}), bf16[16,512,3072]{2,1,0:T(8,128)(2,1)}) %all-gather.5.cloned.1.call-update) | async-done | bytes 50331664 | tf_op jit(solution)/shard_map/all_gather | solution.py:82
  475.4 33.4 %convolution_convert_fusion.2 = bf16[8192,384]{1,0:T(8,128)(2,1)} fusion(bf16[8192,3072]{1,0:T(8,128)(2,1)} %bitcast.146, bf16[384,3072]{1,0:T(8,128)(2,1)} %param.24), kind=kOutput, calls=%fused_computation.60 | convolution fusion | flops 19330498560 | bytes 58982400 | tf_op jit(solution)/shard_map/dot_general | solution.py:84
  508.7 16.6 reshape.200
  555.1 21.1 %copy.90 = f32[48,8,16,512]{3,2,1,0:T(8,128)} copy(f32[48,8,16,512]{3,1,2,0:T(8,128)} %bitcast.106) | data formatting | bytes 25165824
  587.8 21.4 %copy.91 = f32[48,8,16,512]{3,2,1,0:T(8,128)} copy(f32[48,8,16,512]{3,1,2,0:T(8,128)} %bitcast.107) | data formatting | bytes 25165824
  627.7 35.0 %fusion.72 = (f32[16,3,512]{2,1,0:T(4,128)S(1)}, f32[16,3,512,512]{2,3,1,0:T(8,128)}) fusion(bf16[16,512,3,128]{1,0,3,2:T(8,128)(2,1)} %bitcast.123, bf16[16,512,3,128]{1,0,3,2:T(8,128)(2,1)} %bitcast.121), kind=kOutput, calls=%fused_computation.126 | convolution fusion | flops 3258974720 | bytes 63012864 | tf_op jit(solution)/shard_map/jvp()/sub | solution.py:37
  662.7 55.8 %fusion.5 = (f32[16,3,512]{2,1,0:T(4,128)S(1)}, bf16[16,3,512,512]{2,3,1,0:T(8,128)(2,1)}, bf16[16,3,512,512]{2,3,1,0:T(8,128)(2,1)}) fusion(f32[16,3,512,512]{2,3,1,0:T(8,128)} %get-tuple-element.49, f32[16,3,512]{2,1,0:T(4,128)S(1)} %multiply_divide_fusion, f32[16,3,512]{2,1,0:T(4,128)S(1)} %get-tuple-element.48, bf16[16,3,128,512]{3,0,2,1:T(8,128)(2,1)} %bitcast.112, ...), kind=kOutput, calls=%fused_computation.8 | convolution fusion | flops 3309281280 | bytes 113541120 | tf_op jit(solution)/shard_map/transpose(jvp(bhqk,bkhd->bqhd))/dot_general | solution.py:38
  718.6 31.9 %convert_bitcast_fusion = f32[16,512,3,128]{1,3,2,0:T(8,128)} fusion(bf16[16,512,3,128]{1,0,3,2:T(8,128)(2,1)} %bitcast.124, f32[16,3,512,512]{2,3,1,0:T(8,128)} %get-tuple-element.49, bf16[16,3,512,512]{2,3,1,0:T(8,128)(2,1)} %get-tuple-element.50, f32[16,3,512]{2,1,0:T(4,128)S(1)} %neg.23, f32[16,3,512]{2,1,0:T(4,128)S(1)} %get-tuple-element.48), kind=kOutput, calls=%fused_computation.46 | convolution fusion | flops 3290431488 | bytes 94568448 | tf_op jit(solution)/shard_map/transpose(jvp(bqhd,bkhd->bhqk))/dot_general | solution.py:36
  750.4 30.7 %convert_bitcast_fusion.1 = f32[16,512,3,128]{1,3,2,0:T(8,128)} fusion(bf16[16,512,3,128]{1,0,3,2:T(8,128)(2,1)S(1)} %bitcast.122, f32[16,3,512,512]{2,3,1,0:T(8,128)} %get-tuple-element.49, bf16[16,3,512,512]{2,3,1,0:T(8,128)(2,1)} %get-tuple-element.50, f32[16,3,512]{2,1,0:T(4,128)S(1)} %neg.23, f32[16,3,512]{2,1,0:T(4,128)S(1)} %get-tuple-element.48), kind=kOutput, calls=%fused_computation.47 | convolution fusion | flops 3290431488 | bytes 94568448 | tf_op jit(solution)/shard_map/transpose(jvp(bqhd,bkhd->bhqk))/dot_general | solution.py:36
  781.2 16.3 copy.86
  797.5 16.5 copy.87
  814.0 16.3 multiply_subtract_fusion
  842.4 22.0 %copy.95 = f32[48,8,16,512]{3,1,2,0:T(8,128)} copy(f32[48,8,16,512]{3,2,1,0:T(8,128)} %bitcast.104) | data formatting | bytes 25165824
  887.0 21.8 %copy.94 = f32[48,8,16,512]{3,1,2,0:T(8,128)} copy(f32[48,8,16,512]{3,2,1,0:T(8,128)} %bitcast.105) | data formatting | bytes 25165824
  919.9 17.9 %convert_bitcast_fusion.2 = bf16[16,512,3,128]{1,3,2,0:T(8,128)(2,1)} fusion(bf16[16,3,512,512]{2,3,1,0:T(8,128)(2,1)} %get-tuple-element.19, bf16[16,3,128,512]{3,0,2,1:T(8,128)(2,1)} %bitcast.113), kind=kOutput, calls=%fused_computation.65 | convolution fusion | flops 3224371200 | bytes 37748736 | tf_op jit(solution)/shard_map/transpose(jvp(bhqk,bkhd->bqhd))/dot_general | solution.py:38
  954.1 17.2 all-reduce.6.cloned.1.call-done
  996.7 40.8 %fusion.82 = f32[8192,3072]{1,0:T(8,128)} fusion(bf16[8192,384]{0,1:T(8,128)(2,1)} %multiply_convert_fusion, bf16[3072,384]{1,0:T(8,128)(2,1)S(1)} %copy-done), kind=kOutput, calls=%fused_computation.128 | convolution fusion | flops 19327352832 | bytes 109314048 | tf_op jit(solution)/shard_map/dot_general | solution.py:100
  1037.5 41.4 %fusion.81 = f32[8192,3072]{1,0:T(8,128)} fusion(bf16[8192,384]{0,1:T(8,128)(2,1)} %multiply_convert_fusion.1, bf16[3072,384]{1,0:T(8,128)(2,1)} %param.18), kind=kOutput, calls=%fused_computation.127 | convolution fusion | flops 19327352832 | bytes 109314048 | tf_op jit(solution)/shard_map/dot_general | solution.py:99
  1078.9 81.7 %add_convert_fusion = bf16[8192,3072]{1,0:T(8,128)(2,1)} fusion(f32[8192,3072]{1,0:T(8,128)} %fusion.81, f32[8192,3072]{1,0:T(8,128)} %fusion.82, bf16[8192,384]{0,1:T(8,128)(2,1)} %bitcast.114, bf16[3072,384]{1,0:T(8,128)(2,1)S(1)} %copy-done.5), kind=kOutput, calls=%fused_computation.1 | convolution fusion | flops 19402850304 | bytes 260308992 | tf_op jit(solution)/shard_map/dot_general | solution.py:101
  1193.1 35.1 %convolution_convert_fusion = bf16[8192,3072]{1,0:T(8,128)(2,1)} fusion(bf16[8192,384]{0,1:T(8,128)(2,1)} %bitcast.119, bf16[384,3072]{1,0:T(8,128)(2,1)S(1)} %copy-done.29), kind=kOutput, calls=%fused_computation.11 | convolution fusion | flops 19352518656 | bytes 58982400 | tf_op jit(solution)/shard_map/dot_general | solution.py:76
  1228.3 28.6 %convolution_convert_fusion.3 = bf16[384,3072]{1,0:T(8,128)(2,1)} fusion(bf16[8192,384]{0,1:T(8,128)(2,1)} %bitcast.120, bf16[8192,3072]{1,0:T(8,128)(2,1)} %bitcast.147), kind=kOutput, calls=%fused_computation.90 | convolution fusion | flops 19328532480 | bytes 58982400 | tf_op jit(solution)/shard_map/dot_general | solution.py:83
  1256.9 34.2 %convolution_convert_fusion.4 = bf16[3072,384]{1,0:T(8,128)(2,1)} fusion(bf16[8192,3072]{1,0:T(8,128)(2,1)} %bitcast.143, bf16[8192,384]{0,1:T(8,128)(2,1)} %bitcast.115), kind=kOutput, calls=%fused_computation.91 | convolution fusion | flops 19328532480 | bytes 58982400 | tf_op jit(solution)/shard_map/dot_general | solution.py:98
  1291.1 34.5 %convolution_convert_fusion.6 = bf16[3072,384]{1,0:T(8,128)(2,1)} fusion(bf16[8192,3072]{1,0:T(8,128)(2,1)} %bitcast.144, bf16[8192,384]{0,1:T(8,128)(2,1)} %multiply_convert_fusion.1), kind=kOutput, calls=%fused_computation.93 | convolution fusion | flops 19328532480 | bytes 58982400 | tf_op jit(solution)/shard_map/dot_general | solution.py:96
  1325.6 79.4 %reduce-scatter.5.cloned.1.call-done = bf16[16,64,3072]{2,1,0:T(8,128)(2,1)} async-done(((bf16[16,512,3072]{2,1,0:T(8,128)(2,1)}), bf16[16,64,3072]{2,1,0:T(8,128)(2,1)}) %reduce-scatter.5.cloned.1.call-update) | async-done | bytes 6291472 | tf_op jit(solution)/shard_map/reduce_scatter | solution.py:103
  1413.6 238.6 %reduce-scatter.3.cloned.1.call-done = bf16[16,64,3072]{2,1,0:T(8,128)(2,1)} async-done(((bf16[16,512,3072]{2,1,0:T(8,128)(2,1)}), bf16[16,64,3072]{2,1,0:T(8,128)(2,1)}) %reduce-scatter.3.cloned.1.call-update) | async-done | bytes 6291472 | tf_op jit(solution)/shard_map/reduce_scatter | solution.py:77
  1652.3 17.1 fusion.28
  1670.3 34.4 %convolution_convert_fusion.5 = bf16[3072,384]{1,0:T(8,128)(2,1)} fusion(bf16[8192,3072]{1,0:T(8,128)(2,1)} %bitcast.145, bf16[8192,384]{0,1:T(8,128)(2,1)} %multiply_convert_fusion), kind=kOutput, calls=%fused_computation.92 | convolution fusion | flops 19328532480 | bytes 58982400 | tf_op jit(solution)/shard_map/dot_general | solution.py:97
  1704.7 18.5 %all-reduce.8.cloned.1.call-done = f32[16,3,3072]{2,0,1:T(8,128)} async-done(((f32[16,3,3072]{2,0,1:T(8,128)}), f32[16,3,3072]{2,0,1:T(8,128)}) %all-reduce.8.cloned.1.call-update) | async-done | bytes 589840 | tf_op jit(solution)/shard_map/psum | solution.py:104
  (132 shorter events, 220.0 us)
Async XLA Ops:
  7.2 242.7 %copy-start = (bf16[3072,384]{1,0:T(8,128)(2,1)S(1)}, bf16[3072,384]{1,0:T(8,128)(2,1)}, u32[]{:S(2)}) copy-start(bf16[3072,384]{1,0:T(8,128)(2,1)} %param.20) | copy-start | bytes 7077892
  7.2 242.6 %all-gather.3.cloned.1.call-start = ((), (), s32[]{:S(2)}) async-start(), calls=%async_computation.2 | async-start | bytes 56623104 | tf_op jit(solution)/shard_map/all_gather | solution.py:63
  16.0 14.5 copy-start.6
  23.3 226.6 %copy-start.30 = (f32[384]{0:T(512)S(1)}, f32[384]{0:T(512)}, u32[]{:S(2)}) copy-start(f32[384]{0:T(512)} %param.21) | copy-start | bytes 4612
  23.3 452.0 %all-gather.5.cloned.1.call-start = ((), (), s32[]{:S(2)}) async-start(), calls=%async_computation.5 | async-start | bytes 56623104 | tf_op jit(solution)/shard_map/all_gather | solution.py:82
  30.6 511.9 %all-reduce.4.cloned.1.call-start = ((), (), s32[]{:S(2)}) async-start(), calls=%async_computation.3 | async-start | bytes 131072 | tf_op jit(solution)/shard_map/psum | solution.py:68
  249.9 27.8 %copy-start.31 = (f32[384]{0:T(512)S(1)}, f32[384]{0:T(512)}, u32[]{:S(2)}) copy-start(f32[384]{0:T(512)} %param.19) | copy-start | bytes 4612
  277.7 29.8 %copy-start.32 = (f32[384]{0:T(512)S(1)}, f32[384]{0:T(512)}, u32[]{:S(2)}) copy-start(f32[384]{0:T(512)} %param.23) | copy-start | bytes 4612
  341.2 630.1 %all-reduce.6.cloned.1.call-start = ((), (), s32[]{:S(2)}) async-start(), calls=%async_computation.6 | async-start | bytes 131072 | tf_op jit(solution)/shard_map/psum | solution.py:92
  525.3 18.2 %copy-start.25 = (f32[384]{0:T(512)S(1)}, f32[384]{0:T(512)}, u32[]{:S(2)}) copy-start(f32[384]{0:T(512)} %param.26) | copy-start | bytes 4612
  543.5 32.7 %copy-start.16 = (f32[1,8192]{1,0:T(1,128)}, f32[1,8192]{1,0:T(1,128)S(1)}, u32[]{:S(2)}) copy-start(f32[1,8192]{1,0:T(1,128)S(1)} %get-tuple-element.42) | copy-start | bytes 98308
  555.1 21.1 %copy-start.23 = (f32[384]{0:T(512)S(1)}, f32[384]{0:T(512)}, u32[]{:S(2)}) copy-start(f32[384]{0:T(512)} %param.27) | copy-start | bytes 4612
  587.8 21.4 %copy-start.8 = (f32[512,64]{0,1:T(8,128)S(1)}, f32[512,64]{0,1:T(8,128)}, u32[]{:S(2)}) copy-start(f32[512,64]{0,1:T(8,128)} %get-tuple-element.38) | copy-start | bytes 393220
  587.8 21.4 %copy-start.11 = (f32[512,64]{0,1:T(8,128)S(1)}, f32[512,64]{0,1:T(8,128)}, u32[]{:S(2)}) copy-start(f32[512,64]{0,1:T(8,128)} %copy-done.10) | copy-start | bytes 393220
  718.5 31.9 %copy-start.2 = (bf16[16,512,3,64,2]{1,0,4,3,2:T(8,128)(2,1)S(1)}, bf16[16,512,3,64,2]{1,0,4,3,2:T(8,128)(2,1)}, u32[]{:S(2)}) copy-start(bf16[16,512,3,64,2]{1,0,4,3,2:T(8,128)(2,1)} %get-tuple-element.52) | copy-start | bytes 18874372
  797.5 16.5 copy-start.9
  797.5 16.5 copy-start.13
  842.4 22.0 %copy-start.17 = (f32[1,8192]{1,0:T(1,128)S(1)}, f32[1,8192]{1,0:T(1,128)}, u32[]{:S(2)}) copy-start(f32[1,8192]{1,0:T(1,128)} %copy-done.16) | copy-start | bytes 98308
  842.4 22.0 %copy-start.24 = (f32[384]{0:T(512)S(1)}, f32[384]{0:T(512)}, u32[]{:S(2)}) copy-start(f32[384]{0:T(512)} %param.27) | copy-start | bytes 4612
  887.0 21.8 %copy-start.15 = (f32[1,8192]{1,0:T(1,128)S(1)}, f32[1,8192]{1,0:T(1,128)}, u32[]{:S(2)}) copy-start(f32[1,8192]{1,0:T(1,128)} %copy-done.14) | copy-start | bytes 98308
  887.0 21.8 %copy-start.26 = (f32[384]{0:T(512)S(1)}, f32[384]{0:T(512)}, u32[]{:S(2)}) copy-start(f32[384]{0:T(512)} %param.26) | copy-start | bytes 4612
  919.9 485.1 %reduce-scatter.5.cloned.1.call-start = ((), (), s32[]{:S(2)}) async-start(), calls=%async_computation.7 | async-start | bytes 56623104 | tf_op jit(solution)/shard_map/reduce_scatter | solution.py:103
  1037.5 41.4 %copy-start.5 = (bf16[3072,384]{1,0:T(8,128)(2,1)S(1)}, bf16[3072,384]{1,0:T(8,128)(2,1)}, u32[]{:S(2)}) copy-start(bf16[3072,384]{1,0:T(8,128)(2,1)} %param.22) | copy-start | bytes 7077892
  1160.7 491.5 %reduce-scatter.3.cloned.1.call-start = ((), (), s32[]{:S(2)}) async-start(), calls=%async_computation.4 | async-start | bytes 56623104 | tf_op jit(solution)/shard_map/reduce_scatter | solution.py:77
  1176.5 16.6 copy-start.29
  1228.2 495.0 %all-reduce.8.cloned.1.call-start = ((), (), s32[]{:S(2)}) async-start(), calls=%async_computation.8 | async-start | bytes 1179648 | tf_op jit(solution)/shard_map/psum | solution.py:104
  1291.1 113.9 %copy-start.4 = (f32[16,3072]{1,0:T(8,128)S(1)}, f32[16,3072]{1,0:T(8,128)}, u32[]{:S(2)}) copy-start(f32[16,3072]{1,0:T(8,128)} %copy-done.3) | copy-start | bytes 589828
  1291.1 113.9 %copy-start.19 = (f32[16,64]{1,0:T(8,128)S(1)}, f32[16,64]{1,0:T(8,128)}, u32[]{:S(2)}) copy-start(f32[16,64]{1,0:T(8,128)} %copy-done.18) | copy-start | bytes 12292
  1291.1 113.9 %copy-start.21 = (f32[16,64]{1,0:T(8,128)S(1)}, f32[16,64]{1,0:T(8,128)}, u32[]{:S(2)}) copy-start(f32[16,64]{1,0:T(8,128)} %copy-done.20) | copy-start | bytes 12292
  1325.6 326.7 %copy-start.7 = (f32[16,3072]{1,0:T(8,128)S(1)}, f32[16,3072]{1,0:T(8,128)}, u32[]{:S(2)}) copy-start(f32[16,3072]{1,0:T(8,128)} %copy-done.6) | copy-start | bytes 589828
  1325.6 326.7 %copy-start.27 = (f32[3072]{0:T(1024)S(1)}, f32[3072]{0:T(1024)}, u32[]{:S(2)}) copy-start(f32[3072]{0:T(1024)} %param.25) | copy-start | bytes 36868
  1670.3 56.6 %copy-start.1 = (bf16[3072,384]{1,0:T(8,128)(2,1)S(1)}, bf16[3072,384]{1,0:T(8,128)(2,1)}, u32[]{:S(2)}) copy-start(bf16[3072,384]{1,0:T(8,128)(2,1)} %param.20) | copy-start | bytes 7077892
  (10 other events, 58.3 us)
Sparse Core Ops, SparseCore 0:
  23.5 226.3 all-gather.2
  252.0 223.2 all-gather.4
  477.7 51.3 all-reduce.3
  920.0 51.3 all-reduce.5
  1160.8 244.1 reduce-scatter.4
  1407.2 245.0 reduce-scatter.2
  1670.4 52.7 all-reduce.7
where the time goes:
time: 1740 us; the launch traced here: 1730 us
  waiting for transfers between devices  705 us (41%)
  matrix products  642 us (37%)
  local copies, waits for them, and re-layouts  190 us (11%)
  other arithmetic  182 us (10%)
    reduce_scatter x1, waiting for transfers between devices, device_step(): lax.psum_scatter(part_sum, 'tp', scatter_dimension=1, tiled=True)  239 us
    all_gather x1, waiting for transfers between devices, device_step(): lax.all_gather(y_loc, 'tp', axis=1, tiled=True).reshape(rows_all, model_dim)  216 us
    all_gather x1, waiting for transfers between devices, device_step(): lax.all_gather((dy_float * gate_row).astype(jnp.bfloat16), 'tp', axis=1,...  134 us
    unnamed x78, local copies, waits for them, and re-layouts  118 us
    dot_general x3, matrix products, attend(): jnp.einsum('bhqk,bkhd->bqhd', attn_probs, v_heads, preferred_element_type...  89.4 us
    dot_general x1, matrix products, device_step(): lax.dot_general(dv_flat, w_v, COL_CONTRACT, preferred_element_type=jnp.fl...  81.7 us
    reduce_scatter x1, waiting for transfers between devices, device_step(): lax.psum_scatter(dy_part, 'tp', scatter_dimension=1, tiled=True)  79.4 us
    dot_general x2, matrix products, attend(): jnp.einsum('bqhd,bkhd->bhqk', q_rot, k_rot, preferred_element_type=jnp.fl...  62.6 us
  transfers between devices with their start and end apart: 7, of which 6 were waited for; matrix products, arithmetic and copies ran while one was open for 24% of the time, Pallas kernels for 0%

commit v1 on v0

v1 whole, which is shorter than its diff:
```python
import functools

import jax
import jax.numpy as jnp
from jax import lax
from jax.experimental import pallas as pl
from jax.experimental.pallas import tpu as pltpu
from jax.sharding import PartitionSpec as P


HEAD_DIM = 128
EPS_NORM = 1e-6
ROPE_BASE = 10000.0
SCALE = HEAD_DIM ** -0.5
LOG2E = 1.4426950408889634
ROW_CONTRACT = (((0,), (0,)), ((), ()))
COL_CONTRACT = (((1,), (1,)), ((), ()))
MESH = pl.DeviceIdType.MESH
CHUNKS = 4
F32 = jnp.float32
BF16 = jnp.bfloat16


def rope_tables(positions):
    half_dim = HEAD_DIM // 2
    side_len = HEAD_DIM // 6
    first_len = half_dim - 2 * side_len
    lane = jnp.arange(HEAD_DIM)
    pair_idx = lane // 2
    section = (pair_idx >= first_len).astype(jnp.int32) + (pair_idx >= first_len + side_len).astype(jnp.int32)
    offset = jnp.where(section == 0, 0, jnp.where(section == 1, first_len, first_len + side_len))
    sec_width = jnp.where(section == 0, first_len, side_len)
    freq_vals = ROPE_BASE ** (-(pair_idx - offset).astype(F32) / sec_width.astype(F32))
    select = jnp.where(section[None, :] == jnp.arange(3)[:, None], freq_vals[None, :], 0.0)
    angles = jnp.sum(positions.astype(F32)[:, :, None] * select[None, :, :], axis=1)
    sign = jnp.where(lane % 2 == 0, -1.0, 1.0).astype(F32)
    return jnp.cos(angles), jnp.sin(angles) * sign[None, :]


def exchange_kernel(n, x_ref, out_ref, slots, send_sem, recv_sem):
    me = lax.axis_index("tp")
    barrier = pltpu.get_barrier_semaphore()
    for step in range(1, n):
        pl.semaphore_signal(barrier, inc=1, device_id={"tp": lax.rem(me + step, n)}, device_id_type=MESH)
    pl.semaphore_wait(barrier, n - 1)
    copies = []
    for step in range(1, n):
        copy = pltpu.make_async_remote_copy(
            src_ref=x_ref, dst_ref=slots.at[step - 1], send_sem=send_sem.at[step - 1], recv_sem=recv_sem.at[step - 1],
            device_id={"tp": lax.rem(me + step, n)}, device_id_type=MESH)
        copy.start()
        copies.append(copy)
    total = x_ref[...]
    for step in range(1, n):
        copies[step - 1].wait()
        total = total + slots[step - 1]
    out_ref[...] = total


def exchange_sum(x, n, cid):
    return pl.pallas_call(
        functools.partial(exchange_kernel, n),
        out_shape=jax.ShapeDtypeStruct(x.shape, x.dtype),
        in_specs=[pl.BlockSpec(memory_space=pltpu.VMEM)],
        out_specs=pl.BlockSpec(memory_space=pltpu.VMEM),
        scratch_shapes=[
            pltpu.VMEM((n - 1,) + x.shape, x.dtype),
            pltpu.SemaphoreType.DMA((n - 1,)),
            pltpu.SemaphoreType.DMA((n - 1,)),
        ],
        compiler_params=pltpu.CompilerParams(collective_id=cid, has_side_effects=True),
        cost_estimate=pl.CostEstimate(flops=4_000_000, bytes_accessed=200_000, transcendentals=0),
        name="exchange_sum",
    )(x)


def attn_kernel(heads, q0, q1, k0, k1, v0, v1, do0, do1, inv_ref, gq_ref, gk_ref, cos_ref, sin_ref,
                o0, o1, dq0, dq1, dk0, dk1, dv0, dv1, st_ref, dg_ref):
    half = q0.shape[1]
    seq = 2 * half
    cos_tab = cos_ref[...]
    sin_tab = sin_ref[...]
    lane = lax.broadcasted_iota(jnp.int32, (seq, HEAD_DIM), 1)
    even = (lane & 1) == 0

    def partner(x):
        return jnp.where(even, pltpu.roll(x, HEAD_DIM - 1, 1), pltpu.roll(x, 1, 1))

    def load(a, b, cols):
        return jnp.concatenate([a[0, :, cols], b[0, :, cols]], axis=0)

    def store(a, b, cols, x):
        a[0, :, cols] = x[:half]
        b[0, :, cols] = x[half:]

    inv_cols = jnp.transpose(inv_ref[0])
    inv_q = inv_cols[:, 0:1]
    inv_k = inv_cols[:, 1:2]

    @pl.when(pl.program_id(0) == 0)
    def _():
        dg_ref[...] = jnp.zeros_like(dg_ref)

    st_q = jnp.zeros((seq, 1), F32)
    st_k = jnp.zeros((seq, 1), F32)
    for h in range(heads):
        cols = slice(h * HEAD_DIM, (h + 1) * HEAD_DIM)
        gq = gq_ref[:, cols]
        gk = gk_ref[:, cols]
        q_hat = load(q0, q1, cols) * inv_q
        k_hat = load(k0, k1, cols) * inv_k
        qg = q_hat * gq
        kg = k_hat * gk
        q_rot = (qg * cos_tab + partner(qg) * sin_tab).astype(BF16)
        k_rot = (kg * cos_tab + partner(kg) * sin_tab).astype(BF16)
        v = load(v0, v1, cols)
        do = load(do0, do1, cols)
        s = lax.dot_general(q_rot, k_rot, COL_CONTRACT, preferred_element_type=F32)
        e = jnp.exp2((s - jnp.max(s, axis=-1, keepdims=True)) * (SCALE * LOG2E))
        p = e * (1.0 / jnp.sum(e, axis=-1, keepdims=True))
        pb = p.astype(BF16)
        store(o0, o1, cols, jnp.dot(pb, v, preferred_element_type=F32).astype(BF16))
        store(dv0, dv1, cols, lax.dot_general(pb, do, ROW_CONTRACT, preferred_element_type=F32).astype(BF16))
        dp = lax.dot_general(do, v, COL_CONTRACT, preferred_element_type=F32)
        t = dp * p
        ds = (t - p * jnp.sum(t, axis=-1, keepdims=True)).astype(BF16)
        dq = jnp.dot(ds, k_rot, preferred_element_type=F32) * SCALE
        dk = lax.dot_general(ds, q_rot, ROW_CONTRACT, preferred_element_type=F32) * SCALE
        dq = dq.astype(BF16).astype(F32)
        dk = dk.astype(BF16).astype(F32)
        dq_hat = dq * cos_tab - partner(dq) * sin_tab
        dk_hat = dk * cos_tab - partner(dk) * sin_tab
        dgq = dq_hat * q_hat
        dgk = dk_hat * k_hat
        dg_ref[0:1, cols] += jnp.sum(dgq, axis=0, keepdims=True)
        dg_ref[1:2, cols] += jnp.sum(dgk, axis=0, keepdims=True)
        st_q += jnp.sum(dgq * gq, axis=-1, keepdims=True)
        st_k += jnp.sum(dgk * gk, axis=-1, keepdims=True)
        store(dq0, dq1, cols, dq_hat * gq * inv_q)
        store(dk0, dk1, cols, dk_hat * gk * inv_k)
    stats = jnp.where(lane == 0, st_q, jnp.where(lane == 1, st_k, 0.0))
    st_ref[0] = jnp.transpose(stats)[:8, :]


def attention(q, k, v, do, inv_rows, g_q, g_k, cos_tab, sin_tab):
    batch, half, cols = q[0].shape
    seq = 2 * half
    heads = cols // HEAD_DIM
    big = pl.BlockSpec((1, half, cols), lambda b: (b, 0, 0))
    row8 = pl.BlockSpec((1, 8, seq), lambda b: (b, 0, 0))
    gain = pl.BlockSpec((1, cols), lambda b: (0, 0))
    tab = pl.BlockSpec((seq, HEAD_DIM), lambda b: (0, 0))
    sds = jax.ShapeDtypeStruct
    shape = (batch, half, cols)
    outs = pl.pallas_call(
        functools.partial(attn_kernel, heads),
        grid=(batch,),
        in_specs=[big] * 8 + [row8, gain, gain, tab, tab],
        out_specs=[big] * 8 + [row8, pl.BlockSpec((8, cols), lambda b: (0, 0))],
        out_shape=[sds(shape, BF16)] * 2 + [sds(shape, F32)] * 4 + [sds(shape, BF16)] * 2
        + [sds((batch, 8, seq), F32), sds((8, cols), F32)],
        compiler_params=pltpu.CompilerParams(dimension_semantics=("arbitrary",), vmem_limit_bytes=56 * 1024 * 1024),
        cost_estimate=pl.CostEstimate(flops=batch * heads * 24 * seq * seq * HEAD_DIM,
                                      bytes_accessed=batch * seq * cols * 24, transcendentals=batch * heads * seq * seq),
        name="attn_fwd_bwd",
    )(*q, *k, *v, *do, inv_rows, g_q[None], g_k[None], cos_tab, sin_tab)
    return outs[0:2], outs[2:4], outs[4:6], outs[6:8], outs[8], outs[9]


def dy_kernel(has_add, *refs):
    if has_add:
        aq, ak, q, k, dv, coef, wq, wk, wv, add, dq_out, dk_out, dy_out = refs
    else:
        aq, ak, q, k, dv, coef, wq, wk, wv, dq_out, dk_out, dy_out = refs
        add = None

    @pl.when(pl.program_id(0) == 0)
    def _():
        coef_cols = jnp.transpose(coef[...])
        dq_out[...] = (aq[...] - q[...] * coef_cols[:, 0:1]).astype(BF16)
        dk_out[...] = (ak[...] - k[...] * coef_cols[:, 1:2]).astype(BF16)

    total = lax.dot_general(dq_out[...], wq[...], COL_CONTRACT, preferred_element_type=F32)
    total += lax.dot_general(dk_out[...], wk[...], COL_CONTRACT, preferred_element_type=F32)
    total += lax.dot_general(dv[...], wv[...], COL_CONTRACT, preferred_element_type=F32)
    if has_add:
        total += add[...].astype(F32)
    dy_out[...] = total.astype(BF16)


def input_grad(aq, ak, q, k, dv, coef, w_q, w_k, w_v, add=None):
    rows, cols = aq.shape
    depth = w_q.shape[0]
    tile = next(t for t in (512, 384, 256, 128) if depth % t == 0)
    whole = pl.BlockSpec((rows, cols), lambda n: (0, 0))
    weight = pl.BlockSpec((tile, cols), lambda n: (n, 0))
    out_tile = pl.BlockSpec((rows, tile), lambda n: (0, n))
    extra = [] if add is None else [add]
    sds = jax.ShapeDtypeStruct
    return pl.pallas_call(
        functools.partial(dy_kernel, add is not None),
        grid=(depth // tile,),
        in_specs=[whole] * 5 + [pl.BlockSpec((8, rows), lambda n: (0, 0))] + [weight] * 3 + [out_tile] * len(extra),
        out_specs=[whole, whole, out_tile],
        out_shape=[sds((rows, cols), BF16), sds((rows, cols), BF16), sds((rows, depth), BF16)],
        compiler_params=pltpu.CompilerParams(dimension_semantics=("arbitrary",), vmem_limit_bytes=48 * 1024 * 1024),
        cost_estimate=pl.CostEstimate(flops=6 * rows * cols * depth, bytes_accessed=rows * (cols * 22 + depth * 2),
                                      transcendentals=0),
        name="input_grad",
    )(aq, ak, q, k, dv, coef, w_q, w_k, w_v, *extra)


def solution(mesh):
    tp_size = mesh.shape['tp']

    def device_step(x_loc, e_loc, m_block, w_q, b_q, w_k, b_k, w_v, b_v, w_o, b_o, g_q, g_k, pos_part, dy_loc):
        batch_size, seq_loc, model_dim = x_loc.shape
        seq_len = seq_loc * tp_size
        cols = w_q.shape[1]
        chunks = CHUNKS
        nb = batch_size // chunks
        half = seq_len // 2
        hrows = nb * half
        parity = lax.axis_index('tp') % 2
        rings = [list(range(0, tp_size, 2)), list(range(1, tp_size, 2))]
        swap = [(i, i ^ 1) for i in range(tp_size)]
        pos_pairs = pos_part.reshape(tp_size // 2, 2, seq_loc, 3)
        pos_pairs = jnp.where(parity == 0, pos_pairs, pos_pairs[:, ::-1])
        cos_tab, sin_tab = rope_tables(pos_pairs.transpose(1, 0, 2, 3).reshape(seq_len, 3))

        mod_rows = m_block[None] + e_loc
        shift_row = mod_rows[:, 0][:, None]
        scale_one = 1.0 + mod_rows[:, 1][:, None]
        gate_row = mod_rows[:, 2][:, None]

        def part(a, i):
            return a[i * nb:(i + 1) * nb]

        def gather(a):
            own = lax.all_gather(a, 'tp', axis=1, tiled=True, axis_index_groups=rings)
            return own, lax.ppermute(own, 'tp', swap)

        def reduce_scatter(a):
            return lax.psum_scatter(a, 'tp', scatter_dimension=1, tiled=True, axis_index_groups=rings)

        def canonical(own, other, axis):
            first = jnp.where(parity == 0, own, other)
            return jnp.concatenate([first, jnp.where(parity == 0, other, own)], axis=axis)

        def norm_parts(x_part):
            x_float = x_part.astype(F32)
            centered = x_float - jnp.mean(x_float, axis=-1, keepdims=True)
            inv_std = lax.rsqrt(jnp.mean(centered * centered, axis=-1, keepdims=True) + EPS_NORM)
            return x_float, centered * inv_std, inv_std

        y_full, d_proj = [], []
        for i in range(chunks):
            x_norm = norm_parts(part(x_loc, i))[1]
            y_full.append(gather((x_norm * part(scale_one, i) + part(shift_row, i)).astype(BF16)))
            d_proj.append(gather((part(dy_loc, i).astype(F32) * part(gate_row, i)).astype(BF16)))

        x_outs, d_xs, d_mods, o_parts, dqs, dks, dvs, dgs = [], [], [], [], [], [], [], []
        projs, d_ys, ys, dps = [], [], [], []
        for i in range(chunks):
            y = [a.reshape(hrows, model_dim) for a in y_full[i]]
            dp = [a.reshape(hrows, model_dim) for a in d_proj[i]]
            q_raw = [jnp.dot(a, w_q, preferred_element_type=F32) + b_q for a in y]
            k_raw = [jnp.dot(a, w_k, preferred_element_type=F32) + b_k for a in y]
            v = [(jnp.dot(a, w_v, preferred_element_type=F32) + b_v).astype(BF16) for a in y]
            sq = [jnp.stack([jnp.sum(a * a, axis=-1), jnp.sum(b * b, axis=-1)]) for a, b in zip(q_raw, k_raw)]
            sq = [a.reshape(2 * nb, half) for a in sq]
            sq = exchange_sum(canonical(sq[0], sq[1], 1), tp_size, 2 * i)
            inv = lax.rsqrt(sq / model_dim + EPS_NORM)
            inv = canonical(inv[:, :half], inv[:, half:], 1).reshape(2, nb, seq_len)
            inv_rows = jnp.pad(inv.transpose(1, 0, 2), ((0, 0), (0, 6), (0, 0)))
            do = [lax.dot_general(a, w_o, COL_CONTRACT, preferred_element_type=F32).astype(BF16) for a in dp]

            def to_heads(pair):
                return [a.reshape(nb, half, cols) for a in pair]

            def to_rows(pair):
                return [a.reshape(hrows, cols) for a in pair]

            o, dq_s, dk_s, dv, st, dg = attention(to_heads(q_raw), to_heads(k_raw), to_heads(v), to_heads(do),
                                                  inv_rows, g_q, g_k, cos_tab, sin_tab)
            o, dq_s, dk_s, dv = to_rows(o), to_rows(dq_s), to_rows(dk_s), to_rows(dv)
            away = lax.ppermute(jnp.dot(o[1], w_o, preferred_element_type=F32).astype(BF16), 'tp', swap)
            part_sum = (jnp.dot(o[0], w_o, preferred_element_type=F32) + away.astype(F32)).astype(BF16)
            projs.append(reduce_scatter(part_sum.reshape(nb, half, model_dim)))
            st = st[:, :2].transpose(1, 0, 2).reshape(2 * nb, seq_len)
            st = exchange_sum(canonical(st[:, :half], st[:, half:], 1), tp_size, 2 * i + 1)
            st = canonical(st[:, :half], st[:, half:], 1).reshape(2, nb, 2, half)
            coef = st * (inv * inv / model_dim).reshape(2, nb, 2, half)
            coef = jnp.pad(coef.transpose(2, 0, 1, 3).reshape(2, 2, hrows), ((0, 0), (0, 6), (0, 0)))
            dq_b, dk_b, away = input_grad(dq_s[1], dk_s[1], q_raw[1], k_raw[1], dv[1], coef[1], w_q, w_k, w_v)
            away = lax.ppermute(away, 'tp', swap)
            dq_a, dk_a, dy_part = input_grad(dq_s[0], dk_s[0], q_raw[0], k_raw[0], dv[0], coef[0], w_q, w_k, w_v, away)
            d_ys.append(reduce_scatter(dy_part.reshape(nb, half, model_dim)))
            ys += y
            dps += dp
            o_parts += o
            dqs += [dq_a, dq_b]
            dks += [dk_a, dk_b]
            dvs += dv
            dgs.append(dg)

        def weight_grad(lefts, rights):
            total = None
            for a, b in zip(lefts, rights):
                term = lax.dot_general(a, b, ROW_CONTRACT, preferred_element_type=F32)
                total = term if total is None else total + term
            return total.astype(BF16)

        d_wo = weight_grad(o_parts, dps)
        d_wq = weight_grad(ys, dqs)
        d_wk = weight_grad(ys, dks)
        d_wv = weight_grad(ys, dvs)

        for i in range(chunks):
            proj, x_part, dy_part = lax.optimization_barrier((projs[i], part(x_loc, i), part(dy_loc, i)))
            proj = proj.astype(F32) + b_o
            x_outs.append((x_part.astype(F32) + part(gate_row, i) * proj).astype(BF16))
            d_gate = jnp.sum(dy_part.astype(F32) * proj, axis=1)
            d_y, x_part, dy_part = lax.optimization_barrier((d_ys[i], part(x_loc, i), part(dy_loc, i)))
            dy_float = dy_part.astype(F32)
            _, x_norm, inv_std = norm_parts(x_part)
            d_y = d_y.astype(F32)
            d_mods.append(jnp.stack([jnp.sum(d_y, axis=1), jnp.sum(d_y * x_norm, axis=1), d_gate], axis=1))
            d_norm = d_y * part(scale_one, i)
            d_xs.append((dy_float + inv_std * (d_norm - jnp.mean(d_norm, axis=-1, keepdims=True)
                                               - x_norm * jnp.mean(d_norm * x_norm, axis=-1, keepdims=True))).astype(BF16))
        d_mod = lax.psum(jnp.concatenate(d_mods, axis=0), 'tp')
        dg = functools.reduce(jnp.add, dgs)
        return (jnp.concatenate(x_outs, axis=0), jnp.concatenate(d_xs, axis=0), d_mod, jnp.sum(d_mod, axis=0),
                d_wq, d_wk, d_wv, d_wo, dg[0], dg[1])

    in_specs = (P('dp', 'tp', None), P('dp', None, None), P(None, None), P(None, 'tp'), P('tp'), P(None, 'tp'), P('tp'),
                P(None, 'tp'), P('tp'), P('tp', None), P(None), P('tp'), P('tp'), P('dp', None), P('dp', 'tp', None))
    out_specs = (P('dp', 'tp', None), P('dp', 'tp', None), P('dp', None, None), P('dp', None), P('dp', 'tp'), P('dp', 'tp'),
                 P('dp', 'tp'), P(('dp', 'tp'), None), P(('dp', 'tp')), P(('dp', 'tp')))
    return jax.shard_map(device_step, mesh=mesh, in_specs=in_specs, out_specs=out_specs, check_vma=False)
```

time: 1740 us -> 1260 us (0.72)
  waiting for transfers between devices: 705 us -> 248 us
  Pallas kernels: 0 us -> 314 us
  local copies, waits for them, and re-layouts: 190 us -> 55 us
  matrix products: 642 us -> 537 us
  other arithmetic: 182 us -> 78.7 us
    reduce_scatter x2 -> x8, waiting for transfers between devices: 318 us -> 0.1 us  [reduce_scatter(): lax.psum_scatter(a, 'tp', scatter_dimension=1, tiled=True, axis_index_gro...]
    pallas_call x0 -> x20, Pallas kernels: none -> 314 us  [the longest x4 125 us: attention(): pl.pallas_call(functools.partial(attn_kernel, heads), grid=(batch,), in_s...]
    all_gather x2 -> x8, waiting for transfers between devices: 350 us -> 178 us  [gather(): own = lax.all_gather(a, 'tp', axis=1, tiled=True, axis_index_groups=rings)]
    unnamed x78 -> x355, local copies, waits for them, and re-layouts: 118 us -> 38.2 us
    dot_general x17 -> x72, matrix products: 607 us -> 537 us  [the longest x32 269 us: weight_grad(): term = lax.dot_general(a, b, ROW_CONTRACT, preferred_element_type=F32)]
    reshape x3 -> x18, local copies, waits for them, and re-layouts: 49.5 us -> 0.31 us  [the longest x2 0.09 us: device_step(): pos_pairs = pos_part.reshape(tp_size // 2, 2, seq_loc, 3)]
    another operation x7 -> x0, other arithmetic: 44.9 us -> none  [the longest x3 30.4 us: rope_rotate(): jnp.stack([even_part * cos_part - odd_part * sin_part, even_part * sin_pa...]
    sub x1 -> x0, matrix products: 35 us -> none  [attend(): attn_probs = jax.nn.softmax(scores, axis=-1).astype(jnp.bfloat16)]
  transfers between devices with their start and end apart: 7 -> 33, of which waited for: 6 -> 7; matrix products, arithmetic and copies ran while one was open for 24% -> 48% of each run, Pallas kernels for 0% -> 25%
where the time goes in v1:
time: 1260 us; the launch traced here: 1250 us
  matrix products  537 us (43%)
  Pallas kernels  314 us (25%)
  waiting for transfers between devices  248 us (20%)
  other arithmetic  78.7 us (6%)
  local copies, waits for them, and re-layouts  55 us (4%)
  between operations  16.6 us (1%)
    dot_general x32, matrix products, weight_grad(): term = lax.dot_general(a, b, ROW_CONTRACT, preferred_element_type=F32)  269 us
    all_gather x8, waiting for transfers between devices, gather(): own = lax.all_gather(a, 'tp', axis=1, tiled=True, axis_index_groups=rings)  178 us
    pallas_call x4, Pallas kernels, attention(): pl.pallas_call(functools.partial(attn_kernel, heads), grid=(batch,), in_s...  125 us
    pallas_call x8, Pallas kernels, input_grad(): pl.pallas_call(functools.partial(dy_kernel, add is not None), grid=(depth...  123 us
    pallas_call x8, Pallas kernels, exchange_sum(): pl.pallas_call(functools.partial(exchange_kernel, n), out_shape=jax.Shape...  66.9 us
    dot_general x8, matrix products, device_step(): q_raw = [jnp.dot(a, w_q, preferred_element_type=F32) + b_q for a in y]  62.8 us
    dot_general x8, matrix products, device_step(): k_raw = [jnp.dot(a, w_k, preferred_element_type=F32) + b_k for a in y]  62.2 us
    dot_general x8, matrix products, device_step(): lax.dot_general(a, w_o, COL_CONTRACT, preferred_element_type=F32)  54.7 us
  transfers between devices with their start and end apart: 33, of which 7 were waited for; matrix products, arithmetic and copies ran while one was open for 48% of the time, Pallas kernels for 25%

profile of v1, /device:TPU:112, one launch (start us, length us, event | category | flops | bytes accessed | tf_op | source)
XLA Modules:
  0.0 1254.3 jit_solution(6155281910163099922)
XLA Ops:
  31.0 52.9 %all-gather.9.cloned.1.call-done = bf16[4,256,3072]{2,1,0:T(8,128)(2,1)} async-done(((bf16[4,64,3072]{2,1,0:T(8,128)(2,1)}), bf16[4,256,3072]{2,1,0:T(8,128)(2,1)}) %all-gather.9.cloned.1.call-update) | async-done | bytes 6291472 | tf_op jit(solution)/shard_map/all_gather | solution.py:240
  84.6 63.7 %all-gather.11.cloned.1.call-done = bf16[4,256,3072]{2,1,0:T(8,128)(2,1)} async-done(((bf16[4,64,3072]{2,1,0:T(8,128)(2,1)}), bf16[4,256,3072]{2,1,0:T(8,128)(2,1)}) %all-gather.11.cloned.1.call-update) | async-done | bytes 6291472 | tf_op jit(solution)/shard_map/all_gather | solution.py:240
  151.0 61.6 %all-gather.13.cloned.1.call-done = bf16[4,256,3072]{2,1,0:T(8,128)(2,1)} async-done(((bf16[4,64,3072]{2,1,0:T(8,128)(2,1)}), bf16[4,256,3072]{2,1,0:T(8,128)(2,1)}) %all-gather.13.cloned.1.call-update) | async-done | bytes 6291472 | tf_op jit(solution)/shard_map/all_gather | solution.py:240
  279.8 31.4 %attn_fwd_bwd.4 = (bf16[4,256,384]{2,1,0:T(8,128)(2,1)}, bf16[4,256,384]{2,1,0:T(8,128)(2,1)}, f32[4,256,384]{2,1,0:T(8,128)}, f32[4,256,384]{2,1,0:T(8,128)}, f...) custom-call(f32[4,256,384]{2,1,0:T(8,128)} %bitcast.528, ...), custom_call_target="tpu_custom_call" | custom-call | flops 9663676416 | bytes 18874368 | tf_op jit(solution)/shard_map/attn_fwd_bwd/pallas_call | solution.py:155
  312.7 8.7 exchange_sum.12
  326.2 15.1 %input_grad.8 = (bf16[1024,384]{1,0:T(8,128)(2,1)S(1)}, bf16[1024,384]{1,0:T(8,128)(2,1)S(1)}, bf16[1024,3072]{1,0:T(8,128)(2,1)}) custom-call(f32[1024,384]{1,0:T(8,128)S(1)} %bitcast.403, f32[1024,384]{1,0:T(8,128)S(1)} %bitcast.404, f32[1024,384]{1,0:T(8,128)} %get-tuple-element.291.refs_2_, f32[1024,384]{1,0:T(8,128)} %get-tuple-element.289.refs_3_, ...), custom_call_target="tpu_custom_call" | custom-call | flops 7247757312 | bytes 14942208 | tf_op jit(solution)/shard_map/input_grad/pallas_call | solution.py:200
  378.9 15.7 %input_grad.9 = (bf16[1024,384]{1,0:T(8,128)(2,1)S(1)}, bf16[1024,384]{1,0:T(8,128)(2,1)S(1)}, bf16[1024,3072]{1,0:T(8,128)(2,1)}) custom-call(f32[1024,384]{1,0:T(8,128)S(1)} %bitcast.393, f32[1024,384]{1,0:T(8,128)S(1)} %bitcast.394, f32[1024,384]{1,0:T(8,128)} %get-tuple-element.295.refs_2_, f32[1024,384]{1,0:T(8,128)} %get-tuple-element.293.refs_3_, ...), custom_call_target="tpu_custom_call" | custom-call | flops 7247757312 | bytes 14942208 | tf_op jit(solution)/shard_map/input_grad/pallas_call | solution.py:200
  428.1 31.1 %attn_fwd_bwd.5 = (bf16[4,256,384]{2,1,0:T(8,128)(2,1)}, bf16[4,256,384]{2,1,0:T(8,128)(2,1)}, f32[4,256,384]{2,1,0:T(8,128)}, f32[4,256,384]{2,1,0:T(8,128)}, f...) custom-call(f32[4,256,384]{2,1,0:T(8,128)} %bitcast.524, ...), custom_call_target="tpu_custom_call" | custom-call | flops 9663676416 | bytes 18874368 | tf_op jit(solution)/shard_map/attn_fwd_bwd/pallas_call | solution.py:155
  474.1 15.0 %input_grad.10 = (bf16[1024,384]{1,0:T(8,128)(2,1)S(1)}, bf16[1024,384]{1,0:T(8,128)(2,1)S(1)}, bf16[1024,3072]{1,0:T(8,128)(2,1)}) custom-call(f32[1024,384]{1,0:T(8,128)S(1)} %bitcast.405, f32[1024,384]{1,0:T(8,128)S(1)} %bitcast.406, f32[1024,384]{1,0:T(8,128)} %get-tuple-element.315.refs_2_, f32[1024,384]{1,0:T(8,128)} %get-tuple-element.313.refs_3_, ...), custom_call_target="tpu_custom_call" | custom-call | flops 7247757312 | bytes 14942208 | tf_op jit(solution)/shard_map/input_grad/pallas_call | solution.py:200
  526.4 15.6 %input_grad.11 = (bf16[1024,384]{1,0:T(8,128)(2,1)S(1)}, bf16[1024,384]{1,0:T(8,128)(2,1)S(1)}, bf16[1024,3072]{1,0:T(8,128)(2,1)}) custom-call(f32[1024,384]{1,0:T(8,128)S(1)} %bitcast.395, f32[1024,384]{1,0:T(8,128)S(1)} %bitcast.396, f32[1024,384]{1,0:T(8,128)} %get-tuple-element.319.refs_2_, f32[1024,384]{1,0:T(8,128)} %get-tuple-element.317.refs_3_, ...), custom_call_target="tpu_custom_call" | custom-call | flops 7247757312 | bytes 14942208 | tf_op jit(solution)/shard_map/input_grad/pallas_call | solution.py:200
  552.9 9.0 exchange_sum.10
  577.2 31.0 %attn_fwd_bwd.6 = (bf16[4,256,384]{2,1,0:T(8,128)(2,1)}, bf16[4,256,384]{2,1,0:T(8,128)(2,1)}, f32[4,256,384]{2,1,0:T(8,128)}, f32[4,256,384]{2,1,0:T(8,128)}, f...) custom-call(f32[4,256,384]{2,1,0:T(8,128)} %bitcast.526, ...), custom_call_target="tpu_custom_call" | custom-call | flops 9663676416 | bytes 18874368 | tf_op jit(solution)/shard_map/attn_fwd_bwd/pallas_call | solution.py:155
  609.7 8.6 exchange_sum.14
  623.2 15.0 %input_grad.12 = (bf16[1024,384]{1,0:T(8,128)(2,1)S(1)}, bf16[1024,384]{1,0:T(8,128)(2,1)S(1)}, bf16[1024,3072]{1,0:T(8,128)(2,1)}) custom-call(f32[1024,384]{1,0:T(8,128)S(1)} %bitcast.407, f32[1024,384]{1,0:T(8,128)S(1)} %bitcast.408, f32[1024,384]{1,0:T(8,128)} %get-tuple-element.307.refs_2_, f32[1024,384]{1,0:T(8,128)} %get-tuple-element.305.refs_3_, ...), custom_call_target="tpu_custom_call" | custom-call | flops 7247757312 | bytes 14942208 | tf_op jit(solution)/shard_map/input_grad/pallas_call | solution.py:200
  674.7 15.6 %input_grad.13 = (bf16[1024,384]{1,0:T(8,128)(2,1)S(1)}, bf16[1024,384]{1,0:T(8,128)(2,1)S(1)}, bf16[1024,3072]{1,0:T(8,128)(2,1)}) custom-call(f32[1024,384]{1,0:T(8,128)S(1)} %bitcast.397, f32[1024,384]{1,0:T(8,128)S(1)} %bitcast.398, f32[1024,384]{1,0:T(8,128)} %get-tuple-element.311.refs_2_, f32[1024,384]{1,0:T(8,128)} %get-tuple-element.309.refs_3_, ...), custom_call_target="tpu_custom_call" | custom-call | flops 7247757312 | bytes 14942208 | tf_op jit(solution)/shard_map/input_grad/pallas_call | solution.py:200
  701.0 9.0 exchange_sum.11
  725.7 31.0 %attn_fwd_bwd.7 = (bf16[4,256,384]{2,1,0:T(8,128)(2,1)}, bf16[4,256,384]{2,1,0:T(8,128)(2,1)}, f32[4,256,384]{2,1,0:T(8,128)}, f32[4,256,384]{2,1,0:T(8,128)}, f...) custom-call(f32[4,256,384]{2,1,0:T(8,128)} %bitcast.529, ...), custom_call_target="tpu_custom_call" | custom-call | flops 9663676416 | bytes 18874368 | tf_op jit(solution)/shard_map/attn_fwd_bwd/pallas_call | solution.py:155
  770.2 15.3 %input_grad.14 = (bf16[1024,384]{1,0:T(8,128)(2,1)S(1)}, bf16[1024,384]{1,0:T(8,128)(2,1)S(1)}, bf16[1024,3072]{1,0:T(8,128)(2,1)}) custom-call(f32[1024,384]{1,0:T(8,128)S(1)} %bitcast.401, f32[1024,384]{1,0:T(8,128)S(1)} %bitcast.402, f32[1024,384]{1,0:T(8,128)} %get-tuple-element.299.refs_2_, f32[1024,384]{1,0:T(8,128)} %get-tuple-element.297.refs_3_, ...), custom_call_target="tpu_custom_call" | custom-call | flops 7247757312 | bytes 14942208 | tf_op jit(solution)/shard_map/input_grad/pallas_call | solution.py:200
  786.5 10.3 collective-permute-done.15.refs_9_
  799.5 15.6 %input_grad.15 = (bf16[1024,384]{1,0:T(8,128)(2,1)S(1)}, bf16[1024,384]{1,0:T(8,128)(2,1)S(1)}, bf16[1024,3072]{1,0:T(8,128)(2,1)}) custom-call(f32[1024,384]{1,0:T(8,128)S(1)} %bitcast.399, f32[1024,384]{1,0:T(8,128)S(1)} %bitcast.400, f32[1024,384]{1,0:T(8,128)} %get-tuple-element.303.refs_2_, f32[1024,384]{1,0:T(8,128)} %get-tuple-element.301.refs_3_, ...), custom_call_target="tpu_custom_call" | custom-call | flops 7247757312 | bytes 14942208 | tf_op jit(solution)/shard_map/input_grad/pallas_call | solution.py:200
  822.1 10.0 collective-permute-done.5
  842.6 10.0 collective-permute-done.8
  876.5 9.2 fusion.104
  902.7 8.6 fusion.97
  975.2 8.7 fusion.113
  1009.0 9.0 fusion.111
  1027.9 18.2 %fusion = bf16[384,3072]{1,0:T(8,128)(2,1)} fusion(f32[384,3072,1]{1,0,2:T(8,128)} %fusion.123, f32[384,3072,1]{1,0,2:T(8,128)} %fusion.122, f32[384,3072,1]{1,0,2:T(8,128)} %fusion.121, f32[384,3072,1]{1,0,2:T(8,128)} %fusion.120, f32[384,3072,1]{1,0,2:T(8,128)} %fusion.119, f32[384,3072,1]{1,0,2:T(8,128)} %fusion.118, f32[384,3072,1]{1,0,2:T(8,128)} %fusion.117, ...), kind=kOutput, calls=%fused_computation.23 | convolution fusion | flops 2425356288 | bytes 42467328 | tf_op jit(solution)/shard_map/dot_general | solution.py:310
  1046.1 18.9 %fusion.1 = bf16[3072,384]{1,0:T(8,128)(2,1)} fusion(f32[3072,384,1]{1,0,2:T(8,128)} %fusion.116, f32[3072,384,1]{1,0,2:T(8,128)} %fusion.115, f32[3072,384,1]{1,0,2:T(8,128)} %fusion.114, f32[3072,384,1]{1,0,2:T(8,128)} %fusion.113, f32[3072,384,1]{1,0,2:T(8,128)} %fusion.112, f32[3072,384,1]{1,0,2:T(8,128)} %fusion.111, f32[3072,384,1]{1,0,2:T(8,128)} %fusion.110, ...), kind=kOutput, calls=%fused_computation.31 | convolution fusion | flops 2425356288 | bytes 42467328 | tf_op jit(solution)/shard_map/dot_general | solution.py:310
  1072.7 8.7 fusion.103
  1121.9 19.0 %add_convert_fusion.4 = bf16[3072,384]{1,0:T(8,128)(2,1)} fusion(f32[3072,384]{1,0:T(8,128)} %fusion.109, f32[3072,384]{1,0:T(8,128)} %fusion.108, f32[3072,384]{1,0:T(8,128)} %fusion.107, f32[3072,384]{1,0:T(8,128)} %fusion.106, f32[3072,384]{1,0:T(8,128)} %fusion.105, f32[3072,384]{1,0:T(8,128)} %fusion.103, f32[3072,384]{1,0:T(8,128)} %fusion.104, ...), kind=kOutput, calls=%fused_computation.38 | convolution fusion | flops 2425356288 | bytes 42467328 | tf_op jit(solution)/shard_map/dot_general | solution.py:310
  1140.9 18.6 %add_convert_fusion.5 = bf16[3072,384]{1,0:T(8,128)(2,1)} fusion(f32[3072,384]{1,0:T(8,128)} %fusion.102, f32[3072,384]{1,0:T(8,128)} %fusion.101, f32[3072,384]{1,0:T(8,128)} %fusion.100, f32[3072,384]{1,0:T(8,128)} %fusion.99, f32[3072,384]{1,0:T(8,128)} %fusion.98, f32[3072,384]{1,0:T(8,128)} %fusion.96, f32[3072,384]{1,0:T(8,128)} %fusion.97, ...), kind=kOutput, calls=%fused_computation.39 | convolution fusion | flops 2425356288 | bytes 42467328 | tf_op jit(solution)/shard_map/dot_general | solution.py:310
  1207.8 35.8 %all-reduce.10.cloned.1.call-done = f32[16,3,3072]{2,0,1:T(8,128)} async-done(((f32[16,3,3072]{2,0,1:T(8,128)}), f32[16,3,3072]{2,0,1:T(8,128)}) %all-reduce.10.cloned.1.call-update) | async-done | bytes 589840 | tf_op jit(solution)/shard_map/psum | solution.py:332
  (667 shorter events, 591.6 us)
Async XLA Ops:
  7.2 76.7 %all-gather.9.cloned.1.call-start = ((), (), s32[]{:S(2)}) async-start(), calls=%async_computation.8 | async-start | bytes 7864320 | tf_op jit(solution)/shard_map/all_gather | solution.py:240
  19.3 128.9 %all-gather.11.cloned.1.call-start = ((), (), s32[]{:S(2)}) async-start(), calls=%async_computation.9 | async-start | bytes 7864320 | tf_op jit(solution)/shard_map/all_gather | solution.py:240
  24.4 188.2 %all-gather.13.cloned.1.call-start = ((), (), s32[]{:S(2)}) async-start(), calls=%async_computation.11 | async-start | bytes 7864320 | tf_op jit(solution)/shard_map/all_gather | solution.py:240
  25.2 318.3 %all-gather.15.cloned.1.call-start = ((), (), s32[]{:S(2)}) async-start(), calls=%async_computation.12 | async-start | bytes 7864320 | tf_op jit(solution)/shard_map/all_gather | solution.py:240
  25.8 317.8 %all-gather.17.cloned.1.call-start = ((), (), s32[]{:S(2)}) async-start(), calls=%async_computation.14 | async-start | bytes 7864320 | tf_op jit(solution)/shard_map/all_gather | solution.py:240
  26.5 464.9 %all-gather.19.cloned.1.call-start = ((), (), s32[]{:S(2)}) async-start(), calls=%async_computation.15 | async-start | bytes 7864320 | tf_op jit(solution)/shard_map/all_gather | solution.py:240
  27.1 464.3 %all-gather.21.cloned.1.call-start = ((), (), s32[]{:S(2)}) async-start(), calls=%async_computation.17 | async-start | bytes 7864320 | tf_op jit(solution)/shard_map/all_gather | solution.py:240
  30.9 609.7 %all-gather.23.cloned.1.call-start = ((), (), s32[]{:S(2)}) async-start(), calls=%async_computation.18 | async-start | bytes 7864320 | tf_op jit(solution)/shard_map/all_gather | solution.py:240
  83.9 155.7 %collective-permute-start = (bf16[4,256,3072]{2,1,0:T(8,128)(2,1)}, bf16[4,256,3072]{2,1,0:T(8,128)(2,1)}, u32[]{:S(2)}, u32[]{:S(2)}) collective-permute-start(bf16[4,256,3072]{2,1,0:T(8,128)(2,1)} %all-gather.9.cloned.1.call-done), channel_id=1, source_target_pairs={{0,1},{1,0},{2,3},{3,2},{4,5},{5,4},{6,7},{7,6},{8,9},{9,8},{10,11... | collective-permute-start | bytes 18874376 | tf_op jit(solution)/shard_map/ppermute | solution.py:241
  84.0 1075.5 %reduce-scatter.17.cloned.1.call-start = ((), (), s32[]{:S(2)}) async-start(), calls=%async_computation.20 | async-start | bytes 7864320 | tf_op jit(solution)/shard_map/reduce_scatter | solution.py:244
  148.2 124.5 %collective-permute-start.1 = (bf16[4,256,3072]{2,1,0:T(8,128)(2,1)}, bf16[4,256,3072]{2,1,0:T(8,128)(2,1)}, u32[]{:S(2)}, u32[]{:S(2)}) collective-permute-start(bf16[4,256,3072]{2,1,0:T(8,128)(2,1)} %all-gather.11.cloned.1.call-done), channel_id=1, source_target_pairs={{0,1},{1,0},{2,3},{3,2},{4,5},{5,4},{6,7},{7,6},{8,9},{9,8},{10,11... | collective-permute-start | bytes 18874376 | tf_op jit(solution)/shard_map/ppermute | solution.py:241
  212.6 158.3 %collective-permute-start.3 = (bf16[4,256,3072]{2,1,0:T(8,128)(2,1)}, bf16[4,256,3072]{2,1,0:T(8,128)(2,1)}, u32[]{:S(2)}, u32[]{:S(2)}) collective-permute-start(bf16[4,256,3072]{2,1,0:T(8,128)(2,1)} %all-gather.13.cloned.1.call-done), channel_id=1, source_target_pairs={{0,1},{1,0},{2,3},{3,2},{4,5},{5,4},{6,7},{7,6},{8,9},{9,8},{10,11... | collective-permute-start | bytes 18874376 | tf_op jit(solution)/shard_map/ppermute | solution.py:241
  343.1 35.8 %collective-permute-start.12 = (bf16[1024,3072]{1,0:T(8,128)(2,1)}, bf16[1024,3072]{1,0:T(8,128)(2,1)}, u32[]{:S(2)}, u32[]{:S(2)}) collective-permute-start(bf16[1024,3072]{1,0:T(8,128)(2,1)} %get-tuple-element.121), channel_id=1, source_target_pairs={{0,1},{1,0},{2,3},{3,2},{4,5},{5,4},{6,7},{7,6},{8,9},{9,8},{10,11... | collective-permute-start | bytes 18874376 | tf_op jit(solution)/shard_map/ppermute | solution.py:296
  343.5 70.4 %collective-permute-start.4 = (bf16[4,256,3072]{2,1,0:T(8,128)(2,1)}, bf16[4,256,3072]{2,1,0:T(8,128)(2,1)}, u32[]{:S(2)}, u32[]{:S(2)}) collective-permute-start(bf16[4,256,3072]{2,1,0:T(8,128)(2,1)} %all-gather.15.cloned.1.call-done), channel_id=1, source_target_pairs={{0,1},{1,0},{2,3},{3,2},{4,5},{5,4},{6,7},{7,6},{8,9},{9,8},{10,11... | collective-permute-start | bytes 18874376 | tf_op jit(solution)/shard_map/ppermute | solution.py:241
  343.6 174.8 %collective-permute-start.6 = (bf16[4,256,3072]{2,1,0:T(8,128)(2,1)}, bf16[4,256,3072]{2,1,0:T(8,128)(2,1)}, u32[]{:S(2)}, u32[]{:S(2)}) collective-permute-start(bf16[4,256,3072]{2,1,0:T(8,128)(2,1)} %all-gather.17.cloned.1.call-done), channel_id=1, source_target_pairs={{0,1},{1,0},{2,3},{3,2},{4,5},{5,4},{6,7},{7,6},{8,9},{9,8},{10,11... | collective-permute-start | bytes 18874376 | tf_op jit(solution)/shard_map/ppermute | solution.py:241
  396.5 762.9 %reduce-scatter.19.cloned.1.call-start = ((), (), s32[]{:S(2)}) async-start(), calls=%async_computation.21 | async-start | bytes 7864320 | tf_op jit(solution)/shard_map/reduce_scatter | solution.py:244
  490.9 35.5 %collective-permute-start.13 = (bf16[1024,3072]{1,0:T(8,128)(2,1)}, bf16[1024,3072]{1,0:T(8,128)(2,1)}, u32[]{:S(2)}, u32[]{:S(2)}) collective-permute-start(bf16[1024,3072]{1,0:T(8,128)(2,1)} %get-tuple-element.133), channel_id=1, source_target_pairs={{0,1},{1,0},{2,3},{3,2},{4,5},{5,4},{6,7},{7,6},{8,9},{9,8},{10,11... | collective-permute-start | bytes 18874376 | tf_op jit(solution)/shard_map/ppermute | solution.py:296
  491.3 72.0 %collective-permute-start.7 = (bf16[4,256,3072]{2,1,0:T(8,128)(2,1)}, bf16[4,256,3072]{2,1,0:T(8,128)(2,1)}, u32[]{:S(2)}, u32[]{:S(2)}) collective-permute-start(bf16[4,256,3072]{2,1,0:T(8,128)(2,1)} %all-gather.19.cloned.1.call-done), channel_id=1, source_target_pairs={{0,1},{1,0},{2,3},{3,2},{4,5},{5,4},{6,7},{7,6},{8,9},{9,8},{10,11... | collective-permute-start | bytes 18874376 | tf_op jit(solution)/shard_map/ppermute | solution.py:241
  491.4 175.5 %collective-permute-start.9 = (bf16[4,256,3072]{2,1,0:T(8,128)(2,1)}, bf16[4,256,3072]{2,1,0:T(8,128)(2,1)}, u32[]{:S(2)}, u32[]{:S(2)}) collective-permute-start(bf16[4,256,3072]{2,1,0:T(8,128)(2,1)} %all-gather.21.cloned.1.call-done), channel_id=1, source_target_pairs={{0,1},{1,0},{2,3},{3,2},{4,5},{5,4},{6,7},{7,6},{8,9},{9,8},{10,11... | collective-permute-start | bytes 18874376 | tf_op jit(solution)/shard_map/ppermute | solution.py:241
  543.9 615.6 %reduce-scatter.21.cloned.1.call-start = ((), (), s32[]{:S(2)}) async-start(), calls=%async_computation.22 | async-start | bytes 7864320 | tf_op jit(solution)/shard_map/reduce_scatter | solution.py:244
  640.0 34.7 %collective-permute-start.14 = (bf16[1024,3072]{1,0:T(8,128)(2,1)}, bf16[1024,3072]{1,0:T(8,128)(2,1)}, u32[]{:S(2)}, u32[]{:S(2)}) collective-permute-start(bf16[1024,3072]{1,0:T(8,128)(2,1)} %get-tuple-element.145), channel_id=1, source_target_pairs={{0,1},{1,0},{2,3},{3,2},{4,5},{5,4},{6,7},{7,6},{8,9},{9,8},{10,11... | collective-permute-start | bytes 18874376 | tf_op jit(solution)/shard_map/ppermute | solution.py:296
  640.6 70.8 %collective-permute-start.10 = (bf16[4,256,3072]{2,1,0:T(8,128)(2,1)}, bf16[4,256,3072]{2,1,0:T(8,128)(2,1)}, u32[]{:S(2)}, u32[]{:S(2)}) collective-permute-start(bf16[4,256,3072]{2,1,0:T(8,128)(2,1)} %all-gather.23.cloned.1.call-done), channel_id=1, source_target_pairs={{0,1},{1,0},{2,3},{3,2},{4,5},{5,4},{6,7},{7,6},{8,9},{9,8},{10,11... | collective-permute-start | bytes 18874376 | tf_op jit(solution)/shard_map/ppermute | solution.py:241
  692.2 467.3 %reduce-scatter.23.cloned.1.call-start = ((), (), s32[]{:S(2)}) async-start(), calls=%async_computation.23 | async-start | bytes 7864320 | tf_op jit(solution)/shard_map/reduce_scatter | solution.py:244
  786.4 10.4 collective-permute-start.15
  816.9 342.6 %reduce-scatter.11.cloned.1.call-start = ((), (), s32[]{:S(2)}) async-start(), calls=%async_computation.13 | async-start | bytes 7864320 | tf_op jit(solution)/shard_map/reduce_scatter | solution.py:244
  821.9 10.2 collective-permute-start.5
  837.5 322.0 %reduce-scatter.13.cloned.1.call-start = ((), (), s32[]{:S(2)}) async-start(), calls=%async_computation.16 | async-start | bytes 7864320 | tf_op jit(solution)/shard_map/reduce_scatter | solution.py:244
  858.0 301.5 %reduce-scatter.15.cloned.1.call-start = ((), (), s32[]{:S(2)}) async-start(), calls=%async_computation.19 | async-start | bytes 7864320 | tf_op jit(solution)/shard_map/reduce_scatter | solution.py:244
  867.4 73.2 %collective-permute-start.11 = (bf16[1024,3072]{1,0:T(8,128)(2,1)S(1)}, bf16[1024,3072]{1,0:T(8,128)(2,1)S(1)}, u32[]{:S(2)}, u32[]{:S(2)}) collective-permute-start(bf16[1024,3072]{1,0:T(8,128)(2,1)S(1)} %convolution_convert_fusion), channel_id=1, source_target_pairs={{0,1},{1,0},{2,3},{3,2},{4,5},{5,4},{6,7},{7,6},{8,9},{9,8},{10,11... | collective-permute-start | bytes 18874376 | tf_op jit(solution)/shard_map/ppermute | solution.py:287
  876.2 188.9 %collective-permute-start.2 = (bf16[1024,3072]{1,0:T(8,128)(2,1)}, bf16[1024,3072]{1,0:T(8,128)(2,1)}, u32[]{:S(2)}, u32[]{:S(2)}) collective-permute-start(bf16[1024,3072]{1,0:T(8,128)(2,1)} %convolution_convert_fusion.3), channel_id=1, source_target_pairs={{0,1},{1,0},{2,3},{3,2},{4,5},{5,4},{6,7},{7,6},{8,9},{9,8},{10,11... | collective-permute-start | bytes 18874376 | tf_op jit(solution)/shard_map/ppermute | solution.py:287
  946.0 220.5 %reduce-scatter.9.cloned.1.call-start = ((), (), s32[]{:S(2)}) async-start(), calls=%async_computation.10 | async-start | bytes 7864320 | tf_op jit(solution)/shard_map/reduce_scatter | solution.py:244
  1072.3 171.3 %all-reduce.10.cloned.1.call-start = ((), (), s32[]{:S(2)}) async-start(), calls=%async_computation.24 | async-start | bytes 1179648 | tf_op jit(solution)/shard_map/psum | solution.py:332
  (178 other events, 1682.0 us)
Sparse Core Ops, SparseCore 0:
  19.4 64.4 all-gather.8
  86.0 62.1 all-gather.10
  150.4 62.1 all-gather.12
  214.0 63.5 all-gather.14
  279.6 63.5 all-gather.16
  344.6 62.1 all-gather.18
  408.4 63.5 all-gather.20
  473.5 62.1 all-gather.22
  538.0 61.9 reduce-scatter.16
  602.2 60.9 reduce-scatter.18
  692.3 62.5 reduce-scatter.20
  817.1 60.7 reduce-scatter.22
  880.2 59.5 reduce-scatter.10
  941.9 59.5 reduce-scatter.12
  1004.3 59.5 reduce-scatter.14
  1072.5 61.3 reduce-scatter.8
  1188.9 54.6 all-reduce.9
